TPU v7x, 256 devices: a whole 4x4x8 slice. The times are simulated.
256 devices in a mesh: ctx: 64 (over z, x, core), heads: 4 (over y).
Axes of the slice: x: 4, y: 4, z: 8, core: 2. Of those that a mesh axis runs over, the one named last changes fastest.
Arguments:
- query_rows: bfloat16 [64, 16, 2, 128], P('ctx', 'heads'), may hold values from -6 to 6
- past_keys: bfloat16 [64, 16, 4096, 128], P(None, 'heads', 'ctx'), may hold values from -6 to 6
- past_values: bfloat16 [64, 16, 4096, 128], P(None, 'heads', 'ctx'), may hold values from -6 to 6
- used_length: int32 [64], replicated, may hold values from 2048 to 4096
Outputs:
- read: bfloat16 [64, 16, 2, 128], P('ctx', 'heads')
All inputs are finite; a program needn't handle non-finite values.
Results may differ from a plain program's by a relative error of at most 0.0015.
Values may be sent and summed in bfloat16 or wider, within the bound.
No kernel may reach another device: no remote copies, remote signals or barrier semaphores. Data moves between devices by JAX's collectives and lax.ppermute only.
A program may use at most 64 MiB of HBM per device.

v0:
```python
import jax
import jax.numpy as jnp
from jax import lax
from jax.sharding import Mesh
from jax.sharding import PartitionSpec as P

HEAD_SIZE = 128
CTX = ("ctx_0", "ctx_1", "ctx_2")


def gathered_by_axis(value, axes, dim):
    for axis in reversed(axes):
        value = lax.all_gather(value, axis, axis=dim, tiled=True)
    return value


def body(query_rows, past_keys, past_values, used_length):
    all_queries = gathered_by_axis(query_rows, CTX, 0)
    logit = jnp.einsum(
        "bkgd,bktd->bkgt", all_queries, past_keys, preferred_element_type=jnp.float32
    ) * HEAD_SIZE ** (-0.5)
    positions = lax.axis_index(CTX) * past_keys.shape[2] + jnp.arange(past_keys.shape[2])
    filled = positions[None, :] < used_length[:, None]
    logit = jnp.where(filled[:, None, None, :], logit, -1e30)
    top = jnp.max(logit, axis=-1)
    part = jnp.where(filled[:, None, None, :], jnp.exp(logit - top[..., None]), 0.0)
    weight_sum = jnp.sum(part, axis=-1)
    read_sum = jnp.einsum(
        "bkgt,bktd->bkgd", part, past_values.astype(jnp.float32), precision=lax.Precision.HIGHEST
    )
    tops, sums, parts = (
        lax.all_to_all(top[None], CTX, split_axis=1, concat_axis=0, tiled=True),
        lax.all_to_all(weight_sum[None], CTX, split_axis=1, concat_axis=0, tiled=True),
        lax.all_to_all(read_sum[None], CTX, split_axis=1, concat_axis=0, tiled=True),
    )
    best = jnp.max(tops, axis=0)
    scale = jnp.exp(tops - best)
    weight_own = jnp.sum(sums * scale, axis=0)
    read_own = jnp.sum(parts * scale[..., None], axis=0)
    read = (read_own / weight_own[..., None]).astype(jnp.bfloat16)
    return read


def solution(mesh):
    finer = Mesh(
        mesh.devices.reshape(8, 4, 2, mesh.shape["heads"]), ("ctx_0", "ctx_1", "ctx_2", "heads")
    )
    return jax.shard_map(
        body,
        mesh=finer,
        in_specs=(
            P(CTX, "heads", None, None),
            P(None, "heads", CTX, None),
            P(None, "heads", CTX, None),
            P(),
        ),
        out_specs=P(CTX, "heads", None, None),
        check_vma=False,
    )
```

profile of v0, /device:TPU:1, one launch (start us, length us, event | category | flops | bytes accessed | tf_op | source)
XLA Modules:
  0.0 104.1 jit_solution(3401453398949490919)
XLA Ops:
  0.0 0.7 copy.10
  0.7 4.6 %all_gather.9 = bf16[2,4,2,128]{3,1,2,0:T(4,128)(2,1)S(1)} all-gather(bf16[1,4,2,128]{3,1,2,0:T(4,128)(2,1)S(1)} %copy.10), channel_id=1, replica_groups=mesh['ctx_0'=8,'ctx_1'=4,'ctx_2'=2,'heads'=4] {'ctx_2'}, dimensions={0}, use_global_device_ids=true | all-gather | bytes 6144 | tf_op jit(solution)/shard_map/all_gather | solution.py:13
  5.3 8.9 %all_gather.10 = bf16[8,4,2,128]{3,1,2,0:T(4,128)(2,1)S(1)} all-gather(bf16[2,4,2,128]{3,1,2,0:T(4,128)(2,1)S(1)} %all_gather.9), channel_id=1, replica_groups=mesh['ctx_0'=8,'ctx_1'=4,'ctx_2'=2,'heads'=4] {'ctx_1'}, dimensions={0}, use_global_device_ids=true | all-gather | bytes 20480 | tf_op jit(solution)/shard_map/all_gather | solution.py:13
  14.2 20.8 %all_gather.11 = bf16[64,4,2,128]{3,1,2,0:T(4,128)(2,1)S(1)} all-gather(bf16[8,4,2,128]{3,1,2,0:T(4,128)(2,1)S(1)} %all_gather.10), channel_id=1, replica_groups=mesh['ctx_0'=8,'ctx_1'=4,'ctx_2'=2,'heads'=4] {'ctx_0'}, dimensions={0}, use_global_device_ids=true | all-gather | bytes 147456 | tf_op jit(solution)/shard_map/all_gather | solution.py:13
  35.1 0.7 broadcast_compare_fusion
  35.8 4.6 %fusion.10 = (f32[64,4,2]{2,1,0:T(4,128)S(1)}, f32[64,4,2,64]{3,2,1,0:T(2,128)S(1)}) fusion(bf16[64,4,64,128]{3,2,1,0:T(8,128)(2,1)} %param.5, bf16[64,4,2,128]{3,1,2,0:T(4,128)(2,1)S(1)} %all_gather.11, pred[64,64]{1,0:T(8,128)(4,1)S(1)} %broadcast_compare_fusion), kind=kOutput, calls=%fused_computation.19 | convolution fusion | flops 8486400 | bytes 4462592 | tf_op jit(solution)/shard_map/bkgd,bktd->bkgt/dot_general | solution.py:19
  40.4 0.8 fusion.7
  41.2 1.1 %copy.15 = f32[1,64,4,2]{2,3,0,1:T(2,128)} copy(f32[1,64,4,2]{3,2,1,0:T(4,128)S(1)} %bitcast.33) | data formatting | bytes 4096 | tf_op jit(solution)/shard_map/broadcast_in_dim | solution.py:33
  42.3 16.5 %all-to-all-start.2 = ((f32[1,64,4,2]{2,3,0,1:T(2,128)}), f32[1,64,4,2]{2,3,0,1:T(2,128)S(1)}, u32[]{:S(2)}, u32[]{:S(2)}) async-start(f32[1,64,4,2]{2,3,0,1:T(2,128)} %copy.15), calls=%async_computation.2 | async-start | bytes 131072 | tf_op jit(solution)/shard_map/all_to_all | solution.py:33
  58.9 1.1 %copy.13 = f32[1,64,4,2]{2,3,0,1:T(2,128)} copy(f32[1,64,4,2]{3,2,1,0:T(4,128)S(1)} %bitcast.32) | data formatting | bytes 4096 | tf_op jit(solution)/shard_map/broadcast_in_dim | solution.py:32
  59.9 9.1 %all-to-all-done.2 = f32[1,64,4,2]{2,3,0,1:T(2,128)S(1)} async-done(((f32[1,64,4,2]{2,3,0,1:T(2,128)}), f32[1,64,4,2]{2,3,0,1:T(2,128)S(1)}, u32[]{:S(2)}, u32[]{:S(2)}) %all-to-all-start.2) | async-done | bytes 2080 | tf_op jit(solution)/shard_map/all_to_all | solution.py:33
  69.1 4.4 %all-to-all-start.1 = ((f32[1,64,4,2]{2,3,0,1:T(2,128)}), f32[1,64,4,2]{2,3,0,1:T(2,128)S(1)}, u32[]{:S(2)}, u32[]{:S(2)}) async-start(f32[1,64,4,2]{2,3,0,1:T(2,128)} %copy.13), calls=%async_computation.1 | async-start | bytes 131072 | tf_op jit(solution)/shard_map/all_to_all | solution.py:32
  73.5 5.9 %convolution_bitcast_fusion = f32[1,64,4,2,128]{4,3,2,0,1:T(2,128)} fusion(bf16[64,4,64,128]{3,2,1,0:T(8,128)(2,1)} %param.6, f32[64,4,2,64]{3,2,1,0:T(2,128)S(1)} %get-tuple-element.6, pred[64,64]{1,0:T(8,128)(4,1)S(1)} %broadcast_compare_fusion, f32[64,4,2]{2,1,0:T(4,128)S(1)} %get-tuple-element.5), kind=kOutput, calls=%fused_computation | convolution fusion | flops 50397184 | bytes 4593664 | tf_op jit(solution)/shard_map/bkgt,bktd->bkgd/dot_general | solution.py:28
  79.4 4.4 %all-to-all-done.1 = f32[1,64,4,2]{2,3,0,1:T(2,128)S(1)} async-done(((f32[1,64,4,2]{2,3,0,1:T(2,128)}), f32[1,64,4,2]{2,3,0,1:T(2,128)S(1)}, u32[]{:S(2)}, u32[]{:S(2)}) %all-to-all-start.1) | async-done | bytes 2080 | tf_op jit(solution)/shard_map/all_to_all | solution.py:32
  83.8 6.0 %all-to-all-start = ((f32[1,64,4,2,128]{4,3,2,0,1:T(2,128)}), f32[1,64,4,2,128]{4,3,2,0,1:T(2,128)S(1)}, u32[]{:S(2)}, u32[]{:S(2)}) async-start(f32[1,64,4,2,128]{4,3,2,0,1:T(2,128)} %convolution_bitcast_fusion), calls=%async_computation | async-start | bytes 524288 | tf_op jit(solution)/shard_map/all_to_all | solution.py:34
  89.8 0.1 reduce_max.19
  89.9 0.1 fusion.6
  90.0 0.1 copy.16
  90.1 0.5 copy.14
  90.6 12.5 %all-to-all-done = f32[1,64,4,2,128]{4,3,2,0,1:T(2,128)S(1)} async-done(((f32[1,64,4,2,128]{4,3,2,0,1:T(2,128)}), f32[1,64,4,2,128]{4,3,2,0,1:T(2,128)S(1)}, u32[]{:S(2)}, u32[]{:S(2)}) %all-to-all-start) | async-done | bytes 262176 | tf_op jit(solution)/shard_map/all_to_all | solution.py:34
  103.1 0.3 fusion.1
  103.5 0.7 fusion.8
  (2 shorter events, 0.0 us)
Async XLA Ops:
  42.3 26.8 %all-to-all-start.2 = ((f32[1,64,4,2]{2,3,0,1:T(2,128)}), f32[1,64,4,2]{2,3,0,1:T(2,128)S(1)}, u32[]{:S(2)}, u32[]{:S(2)}) async-start(f32[1,64,4,2]{2,3,0,1:T(2,128)} %copy.15), calls=%async_computation.2 | async-start | bytes 131072 | tf_op jit(solution)/shard_map/all_to_all | solution.py:33
  69.1 14.7 %all-to-all-start.1 = ((f32[1,64,4,2]{2,3,0,1:T(2,128)}), f32[1,64,4,2]{2,3,0,1:T(2,128)S(1)}, u32[]{:S(2)}, u32[]{:S(2)}) async-start(f32[1,64,4,2]{2,3,0,1:T(2,128)} %copy.13), calls=%async_computation.1 | async-start | bytes 131072 | tf_op jit(solution)/shard_map/all_to_all | solution.py:32
  83.8 19.4 %all-to-all-start = ((f32[1,64,4,2,128]{4,3,2,0,1:T(2,128)}), f32[1,64,4,2,128]{4,3,2,0,1:T(2,128)S(1)}, u32[]{:S(2)}, u32[]{:S(2)}) async-start(f32[1,64,4,2,128]{4,3,2,0,1:T(2,128)} %convolution_bitcast_fusion), calls=%async_computation | async-start | bytes 524288 | tf_op jit(solution)/shard_map/all_to_all | solution.py:34
where the time goes:
time: 104 us
  blocking collectives  34.4 us (33%)
  starting transfers between devices  27 us (26%)
  waiting for transfers between devices  26 us (25%)
  matrix products  10.5 us (10%)
  local copies, waits for them, and re-layouts  3.48 us (3%)
  other arithmetic  2.74 us (3%)
    all_gather x3, blocking collectives, gathered_by_axis(): value = lax.all_gather(value, axis, axis=dim, tiled=True)  34.4 us
    all_to_all x1, starting transfers between devices, body(): lax.all_to_all(weight_sum[None], CTX, split_axis=1, concat_axis=0, tiled=...  16.5 us
    all_to_all x1, waiting for transfers between devices, body(): lax.all_to_all(read_sum[None], CTX, split_axis=1, concat_axis=0, tiled=True)  12.5 us
    all_to_all x1, waiting for transfers between devices, body(): lax.all_to_all(weight_sum[None], CTX, split_axis=1, concat_axis=0, tiled=...  9.1 us
    all_to_all x1, starting transfers between devices, body(): lax.all_to_all(read_sum[None], CTX, split_axis=1, concat_axis=0, tiled=True)  6.03 us
    dot_general x1, matrix products, body(): jnp.einsum('bkgt,bktd->bkgd', part, past_values.astype(jnp.float32), prec...  5.91 us
    dot_general x1, matrix products, body(): jnp.einsum('bkgd,bktd->bkgt', all_queries, past_keys, preferred_element_t...  4.58 us
    all_to_all x1, starting transfers between devices, body(): lax.all_to_all(top[None], CTX, split_axis=1, concat_axis=0, tiled=True)  4.43 us
  transfers between devices with their start and end apart: 3, of which 3 were waited for; matrix products, arithmetic and copies ran while one was open for 8% of the time, Pallas kernels for 0%

commit v1 on v0

v1 whole, which is shorter than its diff:
```python
import jax
import jax.numpy as jnp
from jax import lax
from jax.experimental import pallas as pl
from jax.experimental.pallas import tpu as pltpu
from jax.sharding import PartitionSpec as P

CTX = "ctx"
SCALE = 128 ** -0.5
EMPTY = -30000.0
GROUP_OF = 8


def split3(x):
    first = lax.reduce_precision(x, 5, 10)
    second = lax.reduce_precision(x - first, 5, 10)
    third = (x - first) - second
    return tuple(piece.astype(jnp.float16) for piece in (first, second, third))


def attend_kernel(used_ref, query_ref, key_ref, value_ref, data_ref, stat_ref):
    sequences, rows, _ = query_ref.shape
    spots = key_ref.shape[1]
    length = spots // (rows // 2)
    first = lax.axis_index(CTX) * length
    row_head = lax.broadcasted_iota(jnp.int32, (rows, spots), 0) // 2
    lane = lax.broadcasted_iota(jnp.int32, (rows, spots), 1)
    position = jnp.where(row_head == lane // length, first + lane % length, 1 << 30)
    seq_lane = lax.broadcasted_iota(jnp.int32, (rows, 128), 1)

    def group(step, stats):
        total_log, scale_log = stats
        base = step * GROUP_OF
        logits = []
        for i in range(GROUP_OF):
            b = base + i
            s = lax.dot_general(
                query_ref[b], key_ref[b], (((1,), (1,)), ((), ())),
                preferred_element_type=jnp.float32,
            )
            logits.append(jnp.where(position < used_ref[b], s, -1e30))
        for i in range(GROUP_OF):
            b = base + i
            s = logits[i]
            top = jnp.maximum(jnp.max(s, axis=1, keepdims=True), -1e9)
            part = jnp.exp((s - top) * SCALE)
            weight = jnp.sum(part, axis=1, keepdims=True)
            high = part.astype(jnp.bfloat16)
            low = (part - high.astype(jnp.float32)).astype(jnp.bfloat16)
            both = lax.dot_general(
                jnp.concatenate([high, low], axis=0), value_ref[b], (((1,), (0,)), ((), ())),
                preferred_element_type=jnp.float32,
            )
            read = both[:rows] + both[rows:]
            most = jnp.max(jnp.abs(read), axis=1, keepdims=True)
            some = most > 0.0
            data_ref[b] = (read * jnp.where(some, 1.0 / jnp.where(some, most, 1.0), 0.0)).astype(data_ref.dtype)
            level = top * SCALE
            log_weight = jnp.where(weight > 0.0, level + jnp.log(weight), EMPTY)
            log_scale = jnp.where(some, level + jnp.log(most), EMPTY)
            here = seq_lane == b
            total_log = jnp.where(here, log_weight, total_log)
            scale_log = jnp.where(here, log_scale, scale_log)
        return total_log, scale_log

    zero = jnp.zeros((rows, 128), jnp.float32)
    total_log, scale_log = lax.fori_loop(0, sequences // GROUP_OF, group, (zero, zero))
    stat_ref[0] = total_log
    stat_ref[1] = scale_log


def attend(used_length, queries, keys, values):
    sequences, rows, width = queries.shape
    return pl.pallas_call(
        attend_kernel,
        out_shape=(
            jax.ShapeDtypeStruct((sequences, rows, width), jnp.float32),
            jax.ShapeDtypeStruct((2, rows, 128), jnp.float32),
        ),
        in_specs=[
            pl.BlockSpec(memory_space=pltpu.SMEM),
            pl.BlockSpec(memory_space=pltpu.VMEM),
            pl.BlockSpec(memory_space=pltpu.VMEM),
            pl.BlockSpec(memory_space=pltpu.VMEM),
        ],
        out_specs=(pl.BlockSpec(memory_space=pltpu.VMEM), pl.BlockSpec(memory_space=pltpu.VMEM)),
        cost_estimate=pl.CostEstimate(flops=10**9, bytes_accessed=9 * 2**20, transcendentals=10**5),
        name="attend",
    )(used_length, queries, keys, values)


def body(query_rows, past_keys, past_values, used_length):
    _, heads, group, width = query_rows.shape
    sequences, _, length, _ = past_keys.shape
    rows = heads * group
    own = jnp.broadcast_to(query_rows.reshape(1, rows, width), (sequences, rows, width))
    queries = lax.all_to_all(own, CTX, split_axis=0, concat_axis=0, tiled=True)
    data, stats = attend(
        used_length, queries,
        past_keys.reshape(sequences, heads * length, width),
        past_values.reshape(sequences, heads * length, width),
    )
    logs = stats[:, :, :sequences].transpose(2, 0, 1).reshape(sequences, 2 * rows)
    pieces = jnp.concatenate(split3(logs), axis=1)
    pieces = jnp.pad(pieces, ((0, 0), (0, group * width - pieces.shape[1]))).reshape(sequences, 1, group, width)
    message = jnp.concatenate([data.astype(jnp.float16).reshape(sequences, heads, group, width), pieces], axis=1)
    got = lax.all_to_all(message, CTX, split_axis=0, concat_axis=0, tiled=True)
    data = got[:, :heads].astype(jnp.float32).reshape(sequences, rows, width)
    logs = got[:, heads].astype(jnp.float32).reshape(sequences, group * width)[:, : 6 * rows]
    logs = logs.reshape(sequences, 3, 2, rows)
    logs = logs[:, 0] + logs[:, 1] + logs[:, 2]
    best = jnp.max(logs[:, 0], axis=0)
    weight = jnp.sum(jnp.exp(logs[:, 0] - best), axis=0)
    read = jnp.sum(data * jnp.exp(logs[:, 1] - best)[..., None], axis=0)
    return (read / weight[:, None]).astype(jnp.bfloat16).reshape(1, heads, group, width)


def solution(mesh):
    return jax.shard_map(
        body,
        mesh=mesh,
        in_specs=(
            P(CTX, "heads", None, None),
            P(None, "heads", CTX, None),
            P(None, "heads", CTX, None),
            P(),
        ),
        out_specs=P(CTX, "heads", None, None),
        check_vma=False,
    )
```

time: 104 us -> 53 us (0.51)
  starting transfers between devices: 27 us -> 0 us
  waiting for transfers between devices: 26 us -> 0 us
  matrix products: 10.5 us -> 0 us
  Pallas kernels: 0 us -> 8.61 us
  blocking collectives: 34.4 us -> 39.5 us
  local copies, waits for them, and re-layouts: 3.48 us -> 1.28 us
    all_to_all x0 -> x2, blocking collectives: none -> 39.5 us  [the longest x1 24 us: body(): queries = lax.all_to_all(own, CTX, split_axis=0, concat_axis=0, tiled=True)]
    all_gather x3 -> x0, blocking collectives: 34.4 us -> none  [gathered_by_axis(): value = lax.all_gather(value, axis, axis=dim, tiled=True)]
    all_to_all x3 -> x0, starting transfers between devices: 27 us -> none  [the longest x1 16.5 us: body(): lax.all_to_all(weight_sum[None], CTX, split_axis=1, concat_axis=0, tiled=...]
    all_to_all x3 -> x0, waiting for transfers between devices: 26 us -> none  [the longest x1 12.5 us: body(): lax.all_to_all(read_sum[None], CTX, split_axis=1, concat_axis=0, tiled=True)]
    dot_general x2 -> x0, matrix products: 10.5 us -> none  [the longest x1 5.91 us: body(): jnp.einsum('bkgt,bktd->bkgd', part, past_values.astype(jnp.float32), prec...]
    pallas_call x0 -> x1, Pallas kernels: none -> 8.61 us  [attend(): pl.pallas_call(attend_kernel, out_shape=(jax.ShapeDtypeStruct((sequences,...]
    convert_element_type x1 -> x3, other arithmetic: 0.66 us -> 2.35 us  [the longest x1 0.97 us: body(): data.astype(jnp.float16).reshape(sequences, heads, group, width)]
    broadcast_in_dim x2 -> x1, local copies, waits for them, and re-layouts: 2.2 us -> 0.7 us  [body(): jnp.broadcast_to(query_rows.reshape(1, rows, width), (sequences, rows, wi...]
  transfers between devices with their start and end apart: 3 -> 0, of which waited for: 3 -> 0; matrix products, arithmetic and copies ran while one was open for 8% -> 0% of each run, Pallas kernels for 0% -> 0%
where the time goes in v1:
time: 53 us; the launch traced here: 52.7 us
  blocking collectives  39.5 us (75%)
  Pallas kernels  8.61 us (16%)
  other arithmetic  3.32 us (6%)
  local copies, waits for them, and re-layouts  1.28 us (2%)
    all_to_all x1, blocking collectives, body(): queries = lax.all_to_all(own, CTX, split_axis=0, concat_axis=0, tiled=True)  24 us
    all_to_all x1, blocking collectives, body(): got = lax.all_to_all(message, CTX, split_axis=0, concat_axis=0, tiled=True)  15.5 us
    pallas_call x1, Pallas kernels, attend(): pl.pallas_call(attend_kernel, out_shape=(jax.ShapeDtypeStruct((sequences,...  8.61 us

profile of v1, /device:TPU:1, one launch (start us, length us, event | category | flops | bytes accessed | tf_op | source)
XLA Modules:
  0.0 52.7 jit_solution(15149959972459498538)
XLA Ops:
  0.0 0.7 %broadcast_in_dim.5 = bf16[64,8,128]{2,1,0:T(8,128)(2,1)S(1)} broadcast(bf16[8,128]{1,0:T(8,128)(2,1)} %bitcast.37), dimensions={1,2} | broadcast | bytes 133120 | tf_op jit(solution)/shard_map/broadcast_in_dim | solution.py:96
  0.7 24.0 %all_to_all.10.query_ref = bf16[64,8,128]{2,1,0:T(8,128)(2,1)} all-to-all(bf16[64,8,128]{2,1,0:T(8,128)(2,1)S(1)} %broadcast_in_dim.5), channel_id=1, replica_groups=mesh['ctx'=64,'heads'=4] {'ctx'}, dimensions={0} | all-to-all | bytes 262144 | tf_op jit(solution)/shard_map/all_to_all | solution.py:97
  24.7 8.6 %attend.1 = (f32[64,8,128]{2,1,0:T(8,128)}, f32[2,8,128]{2,1,0:T(8,128)}) custom-call(s32[64]{0:T(128)} %used_ref.1, bf16[64,8,128]{2,1,0:T(8,128)(2,1)} %all_to_all.10.query_ref, bf16[64,256,128]{2,1,0:T(8,128)(2,1)} %bitcast.30, bf16[64,256,128]{2,1,0:T(8,128)(2,1)} %bitcast.31), custom_call_target="tpu_custom_call" | custom-call | flops 1000000000 | bytes 9437184 | tf_op jit(solution)/shard_map/attend/pallas_call | solution.py:74
  33.3 1.0 %convert_element_type.32 = f16[64,8,128]{2,1,0:T(8,128)(2,1)S(1)} convert(f32[64,8,128]{2,1,0:T(8,128)} %get-tuple-element.7) | non-fusion elementwise | flops 65536 | bytes 393216 | tf_op jit(solution)/shard_map/convert_element_type | solution.py:106
  34.3 0.7 %reduce-precision_convert_fusion.1 = (f16[64,16]{0,1:T(8,128)(2,1)S(1)}, f16[64,16]{0,1:T(8,128)(2,1)S(1)}, f16[64,16]{0,1:T(8,128)(2,1)S(1)}) fusion(f32[2,8,128]{2,1,0:T(8,128)} %get-tuple-element.8), kind=kLoop, calls=%fused_computation.11 | loop fusion | flops 7168 | bytes 10240 | tf_op jit(solution)/shard_map/convert_element_type | solution.py:18
  35.0 0.1 copy.6
  35.1 0.2 pad_maximum_fusion
  35.3 15.5 %all_to_all.11 = f16[64,5,2,128]{3,2,1,0:T(2,128)(2,1)S(1)} all-to-all(f16[64,5,2,128]{3,2,1,0:T(2,128)(2,1)S(1)} %pad_maximum_fusion), channel_id=1, replica_groups=mesh['ctx'=64,'heads'=4] {'ctx'}, dimensions={0} | all-to-all | bytes 327680 | tf_op jit(solution)/shard_map/all_to_all | solution.py:107
  50.9 0.1 copy.7
  51.0 0.1 slice_reduce_fusion
  51.2 0.2 fusion.8
  51.3 0.1 sub.31
  51.4 0.1 div.17
  51.5 0.1 subtract_exponential_fusion
  51.6 0.1 copy.8
  51.7 0.3 multiply_reduce_fusion
  52.1 0.7 %fusion.9 = bf16[1,4,2,128]{3,2,1,0:T(2,128)(2,1)} fusion(f32[4,2,128]{2,1,0:T(2,128)S(1)} %multiply_reduce_fusion, f32[4,2]{1,0:T(4,128)S(1)} %div.17), kind=kLoop, calls=%fused_computation.21 | loop fusion | flops 2048 | bytes 6176 | tf_op jit(solution)/shard_map/convert_element_type | solution.py:115
  (5 shorter events, 0.1 us)

commit v2 on v0

v2 whole, which is shorter than its diff:
```python
import jax
import jax.numpy as jnp
from jax import lax
from jax.experimental import pallas as pl
from jax.experimental.pallas import tpu as pltpu
from jax.sharding import PartitionSpec as P

CTX = "ctx"
SCALE = 128 ** -0.5
EMPTY = -30000.0
CHUNK = 16


def split3(x):
    first = jnp.round(x * 2.0) * 0.5
    second = jnp.round((x - first) * 4096.0) * (1.0 / 4096.0)
    return first, second, (x - first) - second


def attend_kernel(
    used_hbm, query_ref, key_hbm, value_hbm, data_ref,
    used_ref, key_ref, value_ref, logit_ref, used_sem, key_sem, value_sem,
):
    sequences, rows, _ = query_ref.shape
    spots = key_ref.shape[1]
    length = spots // (rows // 2)
    chunks = sequences // CHUNK

    def load(source, target, sems, c):
        span = pl.ds(c * CHUNK, CHUNK)
        return pltpu.make_async_copy(source.at[span], target.at[span], sems.at[c])

    lengths = pltpu.make_async_copy(used_hbm, used_ref, used_sem)
    lengths.start()
    for c in range(chunks + 1):
        if c < chunks:
            load(key_hbm, key_ref, key_sem, c).start()
        if c > 0:
            load(value_hbm, value_ref, value_sem, c - 1).start()

    first = lax.axis_index(CTX) * length
    row_head = lax.broadcasted_iota(jnp.int32, (rows, spots), 0) // 2
    lane = lax.broadcasted_iota(jnp.int32, (rows, spots), 1)
    position = jnp.where(row_head == lane // length, first + lane % length, 1 << 30)
    seq_lane = lax.broadcasted_iota(jnp.int32, (rows, 128), 1)

    def score(b):
        s = lax.dot_general(
            query_ref[b], key_ref[b], (((1,), (1,)), ((), ())), preferred_element_type=jnp.float32
        )
        logit_ref[b] = jnp.where(position < used_ref[b], s, -1e30)

    def read(b, total_log, scale_log):
        s = logit_ref[b]
        top = jnp.maximum(jnp.max(s, axis=1, keepdims=True), -1e9)
        part = jnp.exp((s - top) * SCALE)
        weight = jnp.sum(part, axis=1, keepdims=True)
        high = part.astype(jnp.bfloat16)
        low = (part - high.astype(jnp.float32)).astype(jnp.bfloat16)
        both = lax.dot_general(
            jnp.concatenate([high, low], axis=0), value_ref[b], (((1,), (0,)), ((), ())),
            preferred_element_type=jnp.float32,
        )
        total = both[:rows] + both[rows:]
        most = jnp.max(jnp.abs(total), axis=1, keepdims=True)
        some = most > 0.0
        data_ref[b, : rows // 2] = (total * jnp.where(some, 1.0 / jnp.where(some, most, 1.0), 0.0)).reshape(rows // 2, 2, 128)
        level = top * SCALE
        here = seq_lane == b
        total_log = jnp.where(here, jnp.where(weight > 0.0, level + jnp.log(weight), EMPTY), total_log)
        scale_log = jnp.where(here, jnp.where(some, level + jnp.log(most), EMPTY), scale_log)
        return total_log, scale_log

    total_log = scale_log = jnp.zeros((rows, 128), jnp.float32)
    lengths.wait()
    for c in range(chunks + 1):
        if c < chunks:
            load(key_hbm, key_ref, key_sem, c).wait()
        if c > 0:
            load(value_hbm, value_ref, value_sem, c - 1).wait()
        for i in range(CHUNK):
            if c < chunks:
                score(c * CHUNK + i)
            if c > 0:
                total_log, scale_log = read((c - 1) * CHUNK + i, total_log, scale_log)
    pieces = [piece for pair in zip(split3(total_log), split3(scale_log)) for piece in pair]
    pieces += [jnp.zeros((128 - 6 * rows, 128), jnp.float32)]
    stats = jnp.concatenate(pieces, axis=0).T[:sequences]
    data_ref[:, rows // 2] = jnp.broadcast_to(stats[:, None, :], (sequences, 2, 128))


def in_hbm(x):
    return pltpu.with_memory_space_constraint(x, pltpu.HBM)


def attend(used_length, queries, keys, values):
    sequences, rows, width = queries.shape
    vmem = pl.BlockSpec(memory_space=pltpu.VMEM)
    chunks = sequences // CHUNK
    return pl.pallas_call(
        attend_kernel,
        out_shape=jax.ShapeDtypeStruct((sequences, rows // 2 + 1, 2, width), jnp.float32),
        in_specs=[
            pl.BlockSpec(memory_space=pltpu.HBM),
            vmem,
            pl.BlockSpec(memory_space=pltpu.HBM),
            pl.BlockSpec(memory_space=pltpu.HBM),
        ],
        out_specs=vmem,
        scratch_shapes=[
            pltpu.SMEM(used_length.shape, used_length.dtype),
            pltpu.VMEM(keys.shape, keys.dtype),
            pltpu.VMEM(values.shape, values.dtype),
            pltpu.VMEM((sequences, rows, keys.shape[1]), jnp.float32),
            pltpu.SemaphoreType.DMA,
            pltpu.SemaphoreType.DMA((chunks,)),
            pltpu.SemaphoreType.DMA((chunks,)),
        ],
        compiler_params=pltpu.CompilerParams(vmem_limit_bytes=16 * 2**20),
        cost_estimate=pl.CostEstimate(flops=10**9, bytes_accessed=9 * 2**20, transcendentals=10**5),
        name="attend",
    )(in_hbm(used_length), queries, in_hbm(keys), in_hbm(values))


def merge_kernel(got_ref, read_ref):
    sources, rows, _, _ = got_ref.shape
    rows = (rows - 1) * 2
    x = got_ref[:, rows // 2, 0]
    logs = x + pltpu.roll(x, 128 - 2 * rows, 1) + pltpu.roll(x, 128 - 4 * rows, 1)
    lane = lax.broadcasted_iota(jnp.int32, (1, 128), 1)
    best = jnp.max(logs, axis=0, keepdims=True)
    best = jnp.where(lane < rows, best, pltpu.roll(best, rows, 1))
    share = jnp.exp(jnp.where(lane < 2 * rows, logs - best, 0.0))
    total = pltpu.roll(jnp.sum(share, axis=0, keepdims=True), rows, 1)
    factor = jnp.concatenate([share / total, jnp.zeros((128 - sources, 128), jnp.float32)], axis=0).T
    factor = factor[rows : 2 * rows]
    sums = [jnp.zeros((rows, 128), jnp.float32) for _ in range(4)]
    for s in range(sources):
        sums[s % 4] += got_ref[s, : rows // 2].reshape(rows, 128) * factor[:, s : s + 1]
    read_ref[...] = ((sums[0] + sums[1]) + (sums[2] + sums[3])).astype(read_ref.dtype)


def merge(got):
    vmem = pl.BlockSpec(memory_space=pltpu.VMEM)
    return pl.pallas_call(
        merge_kernel,
        out_shape=jax.ShapeDtypeStruct((2 * got.shape[1] - 2, 128), jnp.bfloat16),
        in_specs=[vmem],
        out_specs=vmem,
        compiler_params=pltpu.CompilerParams(vmem_limit_bytes=4 * 2**20),
        name="merge",
    )(got)


def body(query_rows, past_keys, past_values, used_length):
    _, heads, group, width = query_rows.shape
    sequences, _, length, _ = past_keys.shape
    rows = heads * group
    own = jnp.broadcast_to(query_rows.reshape(1, rows, width), (sequences, rows, width))
    queries = lax.all_to_all(own, CTX, split_axis=0, concat_axis=0, tiled=True)
    message = attend(
        used_length, queries,
        past_keys.reshape(sequences, heads * length, width),
        past_values.reshape(sequences, heads * length, width),
    )
    got = lax.all_to_all(message.astype(jnp.float16), CTX, split_axis=0, concat_axis=0, tiled=True).astype(jnp.float32)
    read = merge(got)
    return read.reshape(1, heads, group, width)


def solution(mesh):
    return jax.shard_map(
        body,
        mesh=mesh,
        in_specs=(
            P(CTX, "heads", None, None),
            P(None, "heads", CTX, None),
            P(None, "heads", CTX, None),
            P(),
        ),
        out_specs=P(CTX, "heads", None, None),
        check_vma=False,
    )
```

time: 104 us -> 46.1 us (0.44)
  starting transfers between devices: 27 us -> 0 us
  waiting for transfers between devices: 26 us -> 0 us
  matrix products: 10.5 us -> 0 us
  Pallas kernels: 0 us -> 5.61 us
  blocking collectives: 34.4 us -> 39.4 us
  local copies, waits for them, and re-layouts: 3.48 us -> 0.7 us
  other arithmetic: 2.74 us -> 0.23 us
    all_to_all x0 -> x2, blocking collectives: none -> 39.4 us  [the longest x1 23.9 us: body(): queries = lax.all_to_all(own, CTX, split_axis=0, concat_axis=0, tiled=True)]
    all_gather x3 -> x0, blocking collectives: 34.4 us -> none  [gathered_by_axis(): value = lax.all_gather(value, axis, axis=dim, tiled=True)]
    all_to_all x3 -> x0, starting transfers between devices: 27 us -> none  [the longest x1 16.5 us: body(): lax.all_to_all(weight_sum[None], CTX, split_axis=1, concat_axis=0, tiled=...]
    all_to_all x3 -> x0, waiting for transfers between devices: 26 us -> none  [the longest x1 12.5 us: body(): lax.all_to_all(read_sum[None], CTX, split_axis=1, concat_axis=0, tiled=True)]
    dot_general x2 -> x0, matrix products: 10.5 us -> none  [the longest x1 5.91 us: body(): jnp.einsum('bkgt,bktd->bkgd', part, past_values.astype(jnp.float32), prec...]
    pallas_call x0 -> x2, Pallas kernels: none -> 5.61 us  [the longest x1 4.48 us: attend(): pl.pallas_call(attend_kernel, out_shape=jax.ShapeDtypeStruct((sequences,...]
    broadcast_in_dim x2 -> x1, local copies, waits for them, and re-layouts: 2.2 us -> 0.7 us  [body(): jnp.broadcast_to(query_rows.reshape(1, rows, width), (sequences, rows, wi...]
    reduce_sum x3 -> x0, other arithmetic: 1.22 us -> none  [the longest x1 0.78 us: body(): weight_sum = jnp.sum(part, axis=-1)]
  transfers between devices with their start and end apart: 3 -> 0, of which waited for: 3 -> 0; matrix products, arithmetic and copies ran while one was open for 8% -> 0% of each run, Pallas kernels for 0% -> 0%
where the time goes in v2:
time: 46.1 us; the launch traced here: 45.9 us
  blocking collectives  39.4 us (85%)
  Pallas kernels  5.61 us (12%)
  local copies, waits for them, and re-layouts  0.7 us (2%)
    all_to_all x1, blocking collectives, body(): queries = lax.all_to_all(own, CTX, split_axis=0, concat_axis=0, tiled=True)  23.9 us
    all_to_all x1, blocking collectives, body(): lax.all_to_all(message.astype(jnp.float16), CTX, split_axis=0, concat_axi...  15.5 us
    pallas_call x1, Pallas kernels, attend(): pl.pallas_call(attend_kernel, out_shape=jax.ShapeDtypeStruct((sequences,...  4.48 us
    pallas_call x1, Pallas kernels, merge(): pl.pallas_call(merge_kernel, out_shape=jax.ShapeDtypeStruct((2 * got.shap...  1.13 us

profile of v2, /device:TPU:1, one launch (start us, length us, event | category | flops | bytes accessed | tf_op | source)
XLA Modules:
  0.0 45.9 jit_solution(16007762639787439826)
XLA Ops:
  0.0 0.7 %broadcast_in_dim.8 = bf16[64,8,128]{2,1,0:T(8,128)(2,1)S(1)} broadcast(bf16[8,128]{1,0:T(8,128)(2,1)} %bitcast.6), dimensions={1,2} | broadcast | bytes 133120 | tf_op jit(solution)/shard_map/broadcast_in_dim | solution.py:159
  0.7 23.9 %all_to_all.10.query_ref = bf16[64,8,128]{2,1,0:T(8,128)(2,1)S(1)} all-to-all(bf16[64,8,128]{2,1,0:T(8,128)(2,1)S(1)} %broadcast_in_dim.8), channel_id=1, replica_groups=mesh['ctx'=64,'heads'=4] {'ctx'}, dimensions={0} | all-to-all | bytes 262144 | tf_op jit(solution)/shard_map/all_to_all | solution.py:160
  24.6 4.5 %attend.1 = f32[64,5,2,128]{3,2,1,0:T(2,128)S(1)} custom-call(s32[64]{0:T(128)} %used_hbm.1, bf16[64,8,128]{2,1,0:T(8,128)(2,1)S(1)} %all_to_all.10.query_ref, bf16[64,256,128]{2,1,0:T(8,128)(2,1)} %bitcast.4, bf16[64,256,128]{2,1,0:T(8,128)(2,1)} %bitcast.5), custom_call_target="tpu_custom_call" | custom-call | flops 1000000000 | bytes 9437184 | tf_op jit(solution)/shard_map/attend/pallas_call | solution.py:100
  29.1 0.1 convert_element_type.6
  29.2 15.5 %all_to_all.11 = f16[64,5,2,128]{3,2,1,0:T(2,128)(2,1)S(1)} all-to-all(f16[64,5,2,128]{3,2,1,0:T(2,128)(2,1)S(1)} %convert_element_type.6), channel_id=1, replica_groups=mesh['ctx'=64,'heads'=4] {'ctx'}, dimensions={0} | all-to-all | bytes 327680 | tf_op jit(solution)/shard_map/all_to_all | solution.py:166
  44.7 0.1 convert_element_type.7.got_ref
  44.8 1.1 %merge.1 = bf16[8,128]{1,0:T(8,128)(2,1)} custom-call(f32[64,5,2,128]{3,2,1,0:T(2,128)S(1)} %convert_element_type.7.got_ref), custom_call_target="tpu_custom_call" | custom-call | tf_op jit(solution)/shard_map/merge/pallas_call | solution.py:145
